TPU v7x, 32 devices: a whole 2x2x4 slice. The times are simulated.
32 devices in a mesh: sims: 2 (over x), rows: 4 (over y, core), fields: 4 (over z).
Axes of the slice: x: 2, y: 2, z: 4, core: 2. Of those that a mesh axis runs over, the one named last changes fastest.
Arguments:
- sky_maps: float32 [6, 32, 16384], P('sims', 'rows', 'fields'), parts along dimension 0, may hold values from -7 to 7
- band_cuts: int32 [6], replicated, may hold values from 1 to 8191, as said below
- filters: float32 [3, 32, 16384], P(None, ('rows', 'fields')), may hold values from 0.3 to 3
- wiener: float32 [2, 32, 16384], P(None, ('rows', 'fields')), may hold values from 0.3 to 3
- response: float32 [32, 16384], P(('rows', 'fields')), may hold values from 0.5 to 2
Outputs:
- phi_curl: float32 [4, 32, 16384], P('sims', 'rows', 'fields'), parts along dimension 0
There are 2 independent parts, one for each index of `sims`. A program takes and returns all parts, laid end to end along the dimension named above; an argument that names none is the same for every part. Nothing has to cross between parts.
Inputs may be any that keep to these rules, and one draw needn't show every extreme that they name: `band_cuts`: entries 0, 2 and 4 are the smallest multipole indices of the temperature, polarization and estimate bands and lie below 512; entries 1, 3 and 5 are the largest and are at least 4096.
All inputs are finite; a program needn't handle non-finite values.
Results may differ from a plain program's by a relative error of at most 0.00019.
Values sent between devices are 32-bit elements; how exact they have to be, the bound alone decides.
No kernel may reach another device: no remote copies, remote signals or barrier semaphores. Data moves between devices by JAX's collectives and lax.ppermute only.
A program may use at most 128 MiB of HBM per device.

v0:
```python
import math
import jax
import jax.numpy as jnp
from jax import lax
from jax.sharding import PartitionSpec as P

NC = 16384
exact_mode = lax.Precision.HIGHEST


def split_factor(length):
    best_first = 1
    for divisor in range(1, math.isqrt(length) + 1):
        if length % divisor == 0:
            best_first = divisor
    return (best_first, length // best_first)


def phase_table(left_index, right_index, period, direction):
    product = left_index[:, None] * right_index[None, :] % period
    angles = direction * 2.0 * math.pi / period * product.astype(jnp.float32)
    return (jnp.cos(angles), jnp.sin(angles))


def complex_einsum(formula, data_pair, table_pair):
    data_real, data_imag = data_pair
    table_real, table_imag = table_pair
    real_out = jnp.einsum(formula, data_real, table_real, precision=exact_mode)
    imag_out = jnp.einsum(formula, data_real, table_imag, precision=exact_mode)
    if data_imag is not None:
        real_out = real_out - jnp.einsum(formula, data_imag, table_imag, precision=exact_mode)
        imag_out = imag_out + jnp.einsum(formula, data_imag, table_real, precision=exact_mode)
    return (real_out, imag_out)


def complex_mul(left_pair, right_pair):
    return (
        left_pair[0] * right_pair[0] - left_pair[1] * right_pair[1],
        left_pair[0] * right_pair[1] + left_pair[1] * right_pair[0],
    )


def conj_mul(left_pair, right_pair):
    return (
        left_pair[0] * right_pair[0] + left_pair[1] * right_pair[1],
        left_pair[0] * right_pair[1] - left_pair[1] * right_pair[0],
    )


def row_transform(data_pair, direction):
    batch_len, length, block_width = data_pair[0].shape
    outer_len, inner_len = split_factor(length)
    outer_ids = jnp.arange(outer_len, dtype=jnp.int32)
    inner_ids = jnp.arange(inner_len, dtype=jnp.int32)
    real_in = data_pair[0].reshape(batch_len, outer_len, inner_len, block_width)
    imag_in = None
    if data_pair[1] is not None:
        imag_in = data_pair[1].reshape(batch_len, outer_len, inner_len, block_width)
    middle = complex_einsum(
        "bjmc,jk->bkmc", (real_in, imag_in), phase_table(outer_ids, outer_ids, outer_len, direction)
    )
    twiddle = phase_table(outer_ids, inner_ids, length, direction)
    middle = complex_mul(middle, (twiddle[0][None, :, :, None], twiddle[1][None, :, :, None]))
    result = complex_einsum(
        "bkmc,mq->bqkc", middle, phase_table(inner_ids, inner_ids, inner_len, direction)
    )
    norm_factor = 1.0 if direction < 0 else 1.0 / length
    return (
        result[0].reshape(batch_len, length, block_width) * norm_factor,
        result[1].reshape(batch_len, length, block_width) * norm_factor,
    )


def block_order(groups, fields_count):
    positions = jnp.arange(groups, dtype=jnp.int32)
    blocks = positions % fields_count * (groups // fields_count) + positions // fields_count
    return (positions, blocks)


def column_forward(data_pair, groups, fields_count):
    batch_len, local_rows, total_len = data_pair[0].shape
    block_width = total_len // groups
    positions, blocks = block_order(groups, fields_count)
    column_ids = jnp.arange(block_width, dtype=jnp.int32)
    shaped = (
        data_pair[0].reshape(batch_len, local_rows, groups, block_width),
        data_pair[1].reshape(batch_len, local_rows, groups, block_width),
    )
    middle = complex_einsum("brpc,pk->brkc", shaped, phase_table(blocks, positions, groups, -1.0))
    twiddle = phase_table(positions, column_ids, total_len, -1.0)
    middle = complex_mul(middle, (twiddle[0][None, None], twiddle[1][None, None]))
    result = complex_einsum(
        "brkc,cq->brqk", middle, phase_table(column_ids, column_ids, block_width, -1.0)
    )
    return (
        result[0].reshape(batch_len, local_rows, total_len),
        result[1].reshape(batch_len, local_rows, total_len),
    )


def column_inverse(data_pair, groups, fields_count):
    batch_len, local_rows, total_len = data_pair[0].shape
    block_width = total_len // groups
    positions, blocks = block_order(groups, fields_count)
    column_ids = jnp.arange(block_width, dtype=jnp.int32)
    shaped = (
        data_pair[0].reshape(batch_len, local_rows, block_width, groups),
        data_pair[1].reshape(batch_len, local_rows, block_width, groups),
    )
    middle = complex_einsum(
        "brqk,qc->brkc", shaped, phase_table(column_ids, column_ids, block_width, 1.0)
    )
    twiddle = phase_table(positions, column_ids, total_len, 1.0)
    middle = complex_mul(middle, (twiddle[0][None, None], twiddle[1][None, None]))
    result = complex_einsum("brkc,kp->brpc", middle, phase_table(positions, blocks, groups, 1.0))
    norm_factor = 1.0 / total_len
    return (
        result[0].reshape(batch_len, local_rows, total_len) * norm_factor,
        result[1].reshape(batch_len, local_rows, total_len) * norm_factor,
    )


def body(sky_maps, band_cuts, filters, wiener, response):
    rows_count = lax.axis_size("rows")
    fields_count = lax.axis_size("fields")
    groups = rows_count * fields_count
    local_rows = filters.shape[1]
    total_rows = local_rows * groups
    row_ratio = NC // total_rows

    def forward_columns(stacked):
        return jnp.stack(column_forward((stacked[0], stacked[1]), groups, fields_count))

    def inverse_rows(stacked):
        return jnp.stack(row_transform((stacked[0], stacked[1]), 1.0))

    def inverse_columns(stacked):
        return jnp.stack(column_inverse((stacked[0], stacked[1]), groups, fields_count))

    def to_frequency(stacked):
        batch_len = stacked.shape[1]
        block_width = stacked.shape[3]
        shaped = stacked.reshape(
            2, batch_len, rows_count, fields_count, local_rows, 1, 1, block_width
        )
        arrived = lax.all_to_all(
            lax.all_to_all(shaped, "rows", split_axis=2, concat_axis=5, tiled=True),
            "fields",
            split_axis=3,
            concat_axis=6,
            tiled=True,
        )
        result = forward_columns(arrived.reshape(2, batch_len, local_rows, groups * block_width))
        return result

    def to_space(stacked):
        batch_len = stacked.shape[1]
        block_width = stacked.shape[3] // groups
        shaped = stacked.reshape(
            2, batch_len, 1, 1, local_rows, rows_count, fields_count, block_width
        )
        arrived = lax.all_to_all(
            lax.all_to_all(shaped, "rows", split_axis=5, concat_axis=2, tiled=True),
            "fields",
            split_axis=6,
            concat_axis=3,
            tiled=True,
        )
        result = inverse_rows(arrived.reshape(2, batch_len, total_rows, block_width))
        return result

    slab_spectra = jnp.stack(
        row_transform(
            (lax.all_to_all(sky_maps, "rows", split_axis=2, concat_axis=1, tiled=True), None), -1.0
        )
    )
    sky_spectra = to_frequency(slab_spectra)
    row_ids = lax.axis_index(("rows", "fields")) * local_rows + jnp.arange(
        local_rows, dtype=jnp.int32
    )
    freq_rows = jnp.where(row_ids < total_rows // 2, row_ids, row_ids - total_rows)[:, None]
    column_ids = jnp.arange(NC, dtype=jnp.int32)
    freq_cols = jnp.where(column_ids < NC // 2, column_ids, column_ids - NC)[None, :]
    scaled_rows = row_ratio * freq_rows
    radius_sq = freq_cols * freq_cols + scaled_rows * scaled_rows

    def band_mask(lower_cut, upper_cut):
        inside = (radius_sq >= lower_cut * lower_cut) & (radius_sq <= upper_cut * upper_cut)
        return inside.astype(jnp.float32)

    mask_temp = band_mask(band_cuts[0], band_cuts[1])
    mask_pol = band_mask(band_cuts[2], band_cuts[3])
    mask_out = band_mask(band_cuts[4], band_cuts[5])
    radius_floor = jnp.maximum(radius_sq, 1).astype(jnp.float32)
    cos_two = (freq_cols * freq_cols - scaled_rows * scaled_rows).astype(jnp.float32) / radius_floor
    sin_two = (2 * freq_cols * scaled_rows).astype(jnp.float32) / radius_floor
    along_x = (2 * freq_cols).astype(jnp.float32) / NC
    along_y = (2 * freq_rows).astype(jnp.float32) / total_rows
    raising = (-along_y + 0.0 * along_x, along_x + 0.0 * along_y)
    lowering = (along_y + 0.0 * along_x, along_x + 0.0 * along_y)
    rotation = (cos_two, sin_two)
    temp_modes = (sky_spectra[0, 0], sky_spectra[1, 0])
    stokes_q = (sky_spectra[0, 1], sky_spectra[1, 1])
    stokes_u = (sky_spectra[0, 2], sky_spectra[1, 2])
    e_modes = (
        -(cos_two * stokes_q[0] + sin_two * stokes_u[0]),
        -(cos_two * stokes_q[1] + sin_two * stokes_u[1]),
    )
    b_modes = (
        sin_two * stokes_q[0] - cos_two * stokes_u[0],
        sin_two * stokes_q[1] - cos_two * stokes_u[1],
    )
    temp_weight = mask_temp * filters[0]
    e_weight = mask_pol * filters[1]
    b_weight = mask_pol * filters[2]
    temp_bar = (temp_weight * temp_modes[0], temp_weight * temp_modes[1])
    e_bar = (e_weight * e_modes[0], e_weight * e_modes[1])
    b_bar = (b_weight * b_modes[0], b_weight * b_modes[1])
    grad_temp = complex_mul(raising, (wiener[0] * temp_bar[0], wiener[0] * temp_bar[1]))
    pol_sum = complex_mul((e_bar[0] - b_bar[1], e_bar[1] + b_bar[0]), rotation)
    pol_bar = (-pol_sum[0], -pol_sum[1])
    pol_rot = complex_mul((wiener[1] * e_bar[0], wiener[1] * e_bar[1]), rotation)
    pol_wiener = (-pol_rot[0], -pol_rot[1])
    spin_three = complex_mul(raising, pol_wiener)
    spin_one = complex_mul(lowering, pol_wiener)
    leg_spectra = jnp.stack(
        [
            jnp.stack([temp_bar[0], grad_temp[0], pol_bar[0], spin_three[0], spin_one[0]]),
            jnp.stack([temp_bar[1], grad_temp[1], pol_bar[1], spin_three[1], spin_one[1]]),
        ]
    )
    leg_maps = to_space(inverse_columns(leg_spectra))
    temp_leg = (leg_maps[0, 0], leg_maps[1, 0])
    grad_leg = (leg_maps[0, 1], leg_maps[1, 1])
    pol_leg = (leg_maps[0, 2], leg_maps[1, 2])
    three_leg = (leg_maps[0, 3], leg_maps[1, 3])
    one_leg = (leg_maps[0, 4], leg_maps[1, 4])
    temp_term = complex_mul(temp_leg, grad_leg)
    raise_term = conj_mul(pol_leg, three_leg)
    lower_term = conj_mul(one_leg, pol_leg)
    current = (
        temp_term[0] + 0.5 * (raise_term[0] + lower_term[0]),
        temp_term[1] + 0.5 * (raise_term[1] + lower_term[1]),
    )
    current_rows = jnp.stack(row_transform((current[0][None], current[1][None]), -1.0))
    current_modes = to_frequency(current_rows)
    out_weight = mask_out * response
    estimate_modes = complex_mul(
        lowering, (out_weight * current_modes[0, 0], out_weight * current_modes[1, 0])
    )
    estimate_stack = jnp.stack([estimate_modes[0][None], estimate_modes[1][None]])
    estimate_maps = to_space(inverse_columns(estimate_stack))
    slab_result = estimate_maps[:, 0]
    return lax.all_to_all(slab_result, "rows", split_axis=1, concat_axis=2, tiled=True)


def solution(mesh):
    placed = (
        P("sims", "rows", "fields"),
        P(),
        P(None, ("rows", "fields"), None),
        P(None, ("rows", "fields"), None),
        P(("rows", "fields"), None),
    )
    return jax.shard_map(
        body, mesh=mesh, in_specs=placed, out_specs=P("sims", "rows", "fields"), check_vma=False
    )
```

profile of v0, /device:TPU:0, one launch (start us, length us, event | category | flops | bytes accessed | tf_op | source)
XLA Modules:
  0.0 572.1 jit_solution(2138556085943826780)
XLA Ops:
  0.0 6.7 %copy.84 = f32[3,8,4096]{1,0,2:T(4,128)} copy(f32[3,8,4096]{2,1,0:T(8,128)} %param.5) | data formatting | bytes 786432 | tf_op args[0]
  6.7 7.5 %reshape.1834 = f32[4,1,24576]{2,1,0:T(1,128)} reshape(f32[4096,3,8]{2,1,0:T(4,128)} %bitcast.453) | data formatting | bytes 786432
  14.2 4.3 all-to-all-start
  18.5 7.4 %all-to-all-done = f32[4,1,24576]{2,1,0:T(1,128)S(1)} async-done(((f32[4,1,24576]{2,1,0:T(1,128)}), f32[4,1,24576]{2,1,0:T(1,128)S(1)}, u32[]{:S(2)}, u32[]{:S(2)}) %all-to-all-start) | async-done | bytes 393248 | tf_op jit(solution)/shard_map/all_to_all | solution.py:174
  28.1 8.7 %reshape.1835 = f32[4096,3,8]{2,1,0:T(4,128)} reshape(f32[4,24576]{1,0:T(4,128)S(1)} %reduce) | data formatting | bytes 786432
  36.9 6.9 %copy.170 = f32[3,8,4,1024]{3,2,1,0:T(4,128)S(1)} copy(f32[3,8,4,1024]{1,0,3,2:T(4,128)} %bitcast.452) | data formatting | bytes 786432 | tf_op jit(solution)/shard_map/all_to_all | solution.py:174
  50.1 14.0 %all_to_all.165 = f32[2,3,4,4,2,1,1,1024]{7,4,3,1,6,5,0,2:T(2,128)S(1)} all-to-all(f32[2,3,4,4,2,1,1,1024]{7,4,3,1,6,5,0,2:T(2,128)S(1)} %copy.92), channel_id=1, replica_groups=mesh['sims'=2,'rows'=4,'fields'=4] {'rows'}, dimensions={2} | all-to-all | bytes 1572864 | tf_op jit(solution)/shard_map/all_to_all | solution.py:147
  65.1 5.7 all-to-all-start.2
  78.8 11.8 %all-to-all-done.2 = f32[2,3,1,4,2,4,1,1024]{7,4,5,1,0,6,2,3:T(2,128)S(1)} async-done(((f32[2,3,1,4,2,4,1,1024]{7,4,5,1,0,6,2,3:T(2,128)}), f32[2,3,1,4,2,4,1,1024]{7,4,5,1,0,6,2,3:T(2,128)S(1)}, u32[]{:S(2)}, u32[]{:S(2)}) %all-to-all-start.2) | async-done | bytes 786464 | tf_op jit(solution)/shard_map/all_to_all | solution.py:146
  93.6 18.6 %fusion.24 = f32[1024,3,2,16]{0,3,2,1:T(8,128)S(1)} fusion(f32[16,3,2,1024]{3,0,2,1:T(8,128)S(1)} %convolution_add_fusion.3, f32[16,3,2,1024]{3,0,2,1:T(8,128)S(1)} %convolution_subtract_fusion.3, f32[16,1024]{1,0:T(8,128)S(1)} %get-tuple-element.50, f32[16,1024]{1,0:T(8,128)S(1)} %get-tuple-element.51), kind=kOutput, calls=%fused_computation.27 | convolution fusion | flops 1222934528 | bytes 1310720 | tf_op jit(solution)/shard_map/brkc,cq->brqk/dot_general | solution.py:28
  112.1 19.3 %fusion.22 = f32[1024,3,2,16]{0,3,2,1:T(8,128)} fusion(f32[16,3,2,1024]{3,0,2,1:T(8,128)S(1)} %convolution_add_fusion.3, f32[16,3,2,1024]{3,0,2,1:T(8,128)S(1)} %convolution_subtract_fusion.3, f32[16,1024]{1,0:T(8,128)S(1)} %get-tuple-element.50, f32[16,1024]{1,0:T(8,128)S(1)} %get-tuple-element.51), kind=kOutput, calls=%fused_computation.25 | convolution fusion | flops 1222934528 | bytes 1310720 | tf_op jit(solution)/shard_map/brkc,cq->brqk/dot_general | solution.py:32
  131.4 19.2 %fusion.88 = f32[3,2,1024,16]{2,3,1,0:T(8,128)} fusion(f32[1024,3,2,16]{0,3,2,1:T(8,128)S(1)} %fusion.24, f32[16,3,2,1024]{3,0,2,1:T(8,128)S(1)} %convolution_add_fusion.3, f32[16,3,2,1024]{3,0,2,1:T(8,128)S(1)} %convolution_subtract_fusion.3, f32[16,1024]{1,0:T(8,128)S(1)} %get-tuple-element.50, f32[16,1024]{1,0:T(8,128)S(1)} %get-tuple-element.51), kind=kOutput, calls=%fused_computation.84 | convolution fusion | flops 1223032832 | bytes 1703936 | tf_op jit(solution)/shard_map/brkc,cq->brqk/dot_general | solution.py:31
  155.0 20.8 %fusion.94 = f32[3,2,1024,16]{2,3,1,0:T(8,128)} fusion(f32[1024,3,2,16]{0,3,2,1:T(8,128)} %fusion.22, f32[16,3,2,1024]{3,0,2,1:T(8,128)} %copy-done.6, f32[16,3,2,1024]{3,0,2,1:T(8,128)} %copy-done.5, f32[16,1024]{1,0:T(8,128)} %copy-done.8, f32[16,1024]{1,0:T(8,128)} %copy-done.10), kind=kOutput, calls=%fused_computation.86 | convolution fusion | flops 1223032832 | bytes 1703936 | tf_op jit(solution)/shard_map/brkc,cq->brqk/dot_general | solution.py:29
  195.4 20.3 %fusion.16 = f32[5,2,16,1024]{3,2,1,0:T(8,128)} fusion(f32[5,2,1024,16]{2,3,1,0:T(8,128)} %constant_dynamic-update-slice_fusion), kind=kOutput, calls=%fused_computation.19 | convolution fusion | flops 2027945984 | bytes 1310720 | tf_op jit(solution)/shard_map/brqk,qc->brkc/dot_general | solution.py:28
  219.8 18.7 %fusion.14 = f32[5,2,16,1024]{3,2,1,0:T(8,128)S(1)} fusion(f32[5,2,1024,16]{2,3,1,0:T(8,128)S(1)} %constant_dynamic-update-slice_fusion.5), kind=kOutput, calls=%fused_computation.17 | convolution fusion | flops 2027945984 | bytes 1310720 | tf_op jit(solution)/shard_map/brqk,qc->brkc/dot_general | solution.py:32
  238.5 20.2 %fusion.77 = f32[5,2,16,1024]{3,2,1,0:T(8,128)S(1)} fusion(f32[5,2,16,1024]{3,2,1,0:T(8,128)S(1)} %copy-done.19, f32[5,2,1024,16]{2,3,1,0:T(8,128)} %copy-done.13), kind=kOutput, calls=%fused_computation.75 | convolution fusion | flops 2028109824 | bytes 1966080 | tf_op jit(solution)/shard_map/brqk,qc->brkc/dot_general | solution.py:31
  258.8 18.8 %fusion.80 = f32[5,2,16,1024]{3,2,1,0:T(8,128)S(1)} fusion(f32[5,2,16,1024]{3,2,1,0:T(8,128)S(1)} %fusion.14, f32[5,2,1024,16]{2,3,1,0:T(8,128)S(1)} %copy-done.12), kind=kOutput, calls=%fused_computation.76 | convolution fusion | flops 2028109824 | bytes 1966080 | tf_op jit(solution)/shard_map/brqk,qc->brkc/dot_general | solution.py:29
  281.6 19.7 %all_to_all.166 = f32[2,5,1,1,2,4,4,1024]{7,6,4,1,3,2,0,5:T(4,128)S(1)} all-to-all(f32[2,5,1,1,2,4,4,1024]{7,6,4,1,3,2,0,5:T(4,128)S(1)} %copy.171), channel_id=1, replica_groups=mesh['sims'=2,'rows'=4,'fields'=4] {'rows'}, dimensions={5} | all-to-all | bytes 2621440 | tf_op jit(solution)/shard_map/all_to_all | solution.py:163
  307.0 31.0 %all-to-all-done.4 = f32[2,5,4,1,2,1,4,1024]{7,2,4,1,0,5,3,6:T(4,128)S(1)} async-done(((f32[2,5,4,1,2,1,4,1024]{7,2,4,1,0,5,3,6:T(4,128)}), f32[2,5,4,1,2,1,4,1024]{7,2,4,1,0,5,3,6:T(4,128)S(1)}, u32[]{:S(2)}, u32[]{:S(2)}) %all-to-all-start.4) | async-done | bytes 1310752 | tf_op jit(solution)/shard_map/all_to_all | solution.py:162
  353.2 8.4 %all_to_all.167 = f32[2,1,4,4,2,1,1,1024]{7,4,3,6,5,1,0,2:T(2,128)S(1)} all-to-all(f32[2,1,4,4,2,1,1,1024]{7,4,3,6,5,1,0,2:T(2,128)S(1)} %copy.129), channel_id=1, replica_groups=mesh['sims'=2,'rows'=4,'fields'=4] {'rows'}, dimensions={2} | all-to-all | bytes 524288 | tf_op jit(solution)/shard_map/all_to_all | solution.py:147
  368.1 6.4 %all-to-all-done.6 = f32[2,1,1,4,2,4,1,1024]{7,4,5,0,6,2,1,3:T(2,128)S(1)} async-done(((f32[2,1,1,4,2,4,1,1024]{7,4,5,0,6,2,1,3:T(2,128)}), f32[2,1,1,4,2,4,1,1024]{7,4,5,0,6,2,1,3:T(2,128)S(1)}, u32[]{:S(2)}, u32[]{:S(2)}) %all-to-all-start.6) | async-done | bytes 262176 | tf_op jit(solution)/shard_map/all_to_all | solution.py:146
  376.1 18.3 %fusion.12 = f32[1024,2,16]{0,2,1:T(8,128)S(1)} fusion(f32[16,1,2,1024]{3,0,2,1:T(8,128)S(1)} %fusion.97, f32[16,1,2,1024]{3,0,2,1:T(8,128)S(1)} %fusion.98, f32[16,1024]{1,0:T(8,128)S(1)} %copy-done.9, f32[16,1024]{1,0:T(8,128)S(1)} %copy-done.11), kind=kOutput, calls=%fused_computation.15 | convolution fusion | flops 417431552 | bytes 524288 | tf_op jit(solution)/shard_map/brkc,cq->brqk/dot_general | solution.py:31
  394.4 18.3 %fusion.10 = f32[1024,2,16]{0,2,1:T(8,128)S(1)} fusion(f32[16,1,2,1024]{3,0,2,1:T(8,128)S(1)} %fusion.97, f32[16,1,2,1024]{3,0,2,1:T(8,128)S(1)} %fusion.98, f32[16,1024]{1,0:T(8,128)S(1)} %copy-done.9, f32[16,1024]{1,0:T(8,128)S(1)} %copy-done.11), kind=kOutput, calls=%fused_computation.13 | convolution fusion | flops 417431552 | bytes 524288 | tf_op jit(solution)/shard_map/brkc,cq->brqk/dot_general | solution.py:29
  412.8 18.4 %fusion.114 = f32[1,2,1024,16]{2,3,1,0:T(8,128)S(1)} fusion(f32[1024,2,16]{0,2,1:T(8,128)S(1)} %fusion.12, f32[16,1,2,1024]{3,0,2,1:T(8,128)S(1)} %fusion.97, f32[16,1,2,1024]{3,0,2,1:T(8,128)S(1)} %fusion.98, f32[16,1024]{1,0:T(8,128)S(1)} %copy-done.9, f32[16,1024]{1,0:T(8,128)S(1)} %copy-done.11), kind=kOutput, calls=%fused_computation.110 | convolution fusion | flops 417464320 | bytes 655360 | tf_op jit(solution)/shard_map/brkc,cq->brqk/dot_general | solution.py:28
  432.1 18.2 %fusion.120 = f32[1,2,1024,16]{2,3,1,0:T(8,128)S(1)} fusion(f32[1024,2,16]{0,2,1:T(8,128)S(1)} %fusion.10, f32[16,1,2,1024]{3,0,2,1:T(8,128)S(1)} %fusion.97, f32[16,1,2,1024]{3,0,2,1:T(8,128)S(1)} %fusion.98, f32[16,1024]{1,0:T(8,128)S(1)} %copy-done.9, f32[16,1024]{1,0:T(8,128)S(1)} %copy-done.11), kind=kOutput, calls=%fused_computation.112 | convolution fusion | flops 417464320 | bytes 655360 | tf_op jit(solution)/shard_map/brkc,cq->brqk/dot_general | solution.py:32
  452.0 21.4 %fusion.4 = f32[2,16,1024]{2,1,0:T(8,128)S(1)} fusion(f32[2,1024,16]{2,1,0:T(8,128)S(1)} %reshape.1797), kind=kOutput, calls=%fused_computation.7 | convolution fusion | flops 417333248 | bytes 262144 | tf_op jit(solution)/shard_map/brqk,qc->brkc/dot_general | solution.py:31
  473.8 21.2 %fusion.2 = f32[2,16,1024]{2,1,0:T(8,128)S(1)} fusion(f32[2,1024,16]{2,1,0:T(8,128)S(1)} %reshape.1796), kind=kOutput, calls=%fused_computation.5 | convolution fusion | flops 417333248 | bytes 262144 | tf_op jit(solution)/shard_map/brqk,qc->brkc/dot_general | solution.py:29
  494.9 21.5 %fusion.105 = f32[2,16,1024]{2,1,0:T(8,128)S(1)} fusion(f32[2,16,1024]{2,1,0:T(8,128)S(1)} %fusion.4, f32[2,1024,16]{2,1,0:T(8,128)S(1)} %reshape.1796), kind=kOutput, calls=%fused_computation.107 | convolution fusion | flops 417366016 | bytes 393216 | tf_op jit(solution)/shard_map/brqk,qc->brkc/dot_general | solution.py:28
  516.4 21.1 %fusion.108 = f32[2,16,1024]{2,1,0:T(8,128)S(1)} fusion(f32[2,16,1024]{2,1,0:T(8,128)S(1)} %fusion.2, f32[2,1024,16]{2,1,0:T(8,128)S(1)} %reshape.1797), kind=kOutput, calls=%fused_computation.108 | convolution fusion | flops 417366016 | bytes 393216 | tf_op jit(solution)/shard_map/brqk,qc->brkc/dot_general | solution.py:32
  539.2 8.4 %all_to_all.168 = f32[2,1,1,1,2,4,4,1024]{7,6,4,3,2,1,0,5:T(4,128)S(1)} all-to-all(f32[2,1,1,1,2,4,4,1024]{7,6,4,3,2,1,0,5:T(4,128)S(1)} %copy.172), channel_id=1, replica_groups=mesh['sims'=2,'rows'=4,'fields'=4] {'rows'}, dimensions={5} | all-to-all | bytes 524288 | tf_op jit(solution)/shard_map/all_to_all | solution.py:163
  547.7 11.3 %all_to_all.169 = f32[2,1,4,1,2,1,4,1024]{7,2,4,0,5,3,1,6:T(4,128)S(1)} all-to-all(f32[2,1,4,1,2,1,4,1024]{7,2,4,0,5,3,1,6:T(4,128)S(1)} %copy.141), channel_id=1, replica_groups=mesh['sims'=2,'rows'=4,'fields'=4] {'fields'}, dimensions={6} | all-to-all | bytes 524288 | tf_op jit(solution)/shard_map/all_to_all | solution.py:162
  562.7 8.4 %all_to_all.170 = f32[2,32,1024]{2,0,1:T(2,128)S(1)} all-to-all(f32[2,32,1024]{2,0,1:T(2,128)S(1)} %copy.148), channel_id=1, replica_groups=mesh['sims'=2,'rows'=4,'fields'=4] {'rows'}, dimensions={1} | all-to-all | bytes 524288 | tf_op jit(solution)/shard_map/all_to_all | solution.py:254
  (197 shorter events, 82.4 us)
Async XLA Ops:
  14.2 11.7 %all-to-all-start = ((f32[4,1,24576]{2,1,0:T(1,128)}), f32[4,1,24576]{2,1,0:T(1,128)S(1)}, u32[]{:S(2)}, u32[]{:S(2)}) async-start(f32[4,1,24576]{2,1,0:T(1,128)} %reshape.1834), calls=%async_computation | async-start | bytes 786432 | tf_op jit(solution)/shard_map/all_to_all | solution.py:174
  49.1 21.7 %copy-start.14 = (s32[6]{0:T(128)S(1)}, s32[6]{0:T(128)}, u32[]{:S(2)}) copy-start(s32[6]{0:T(128)} %param.6) | copy-start | bytes 76
  65.1 25.4 %all-to-all-start.2 = ((f32[2,3,1,4,2,4,1,1024]{7,4,5,1,0,6,2,3:T(2,128)}), f32[2,3,1,4,2,4,1,1024]{7,4,5,1,0,6,2,3:T(2,128)S(1)}, u32[]{:S(2)}, u32[]{:S(2)}) async-start(f32[2,3,1,4,2,4,1,1024]{7,4,5,1,0,6,2,3:T(2,128)} %copy.93), calls=%async_computation.2 | async-start | bytes 1572864 | tf_op jit(solution)/shard_map/all_to_all | solution.py:146
  78.4 53.0 %copy-start.8 = (f32[16,1024]{1,0:T(8,128)}, f32[16,1024]{1,0:T(8,128)S(1)}, u32[]{:S(2)}) copy-start(f32[16,1024]{1,0:T(8,128)S(1)} %get-tuple-element.50) | copy-start | bytes 196612
  78.4 53.0 %copy-start.10 = (f32[16,1024]{1,0:T(8,128)}, f32[16,1024]{1,0:T(8,128)S(1)}, u32[]{:S(2)}) copy-start(f32[16,1024]{1,0:T(8,128)S(1)} %get-tuple-element.51) | copy-start | bytes 196612
  78.7 107.7 %copy-start.2 = (s32[16384]{0:T(1024)}, s32[16384]{0:T(1024)S(1)}, u32[]{:S(2)}) copy-start(s32[16384]{0:T(1024)S(1)} %get-tuple-element.54) | copy-start | bytes 196612
  93.0 38.4 %copy-start.5 = (f32[16,3,2,1024]{3,0,2,1:T(8,128)}, f32[16,3,2,1024]{3,0,2,1:T(8,128)S(1)}, u32[]{:S(2)}) copy-start(f32[16,3,2,1024]{3,0,2,1:T(8,128)S(1)} %convolution_subtract_fusion.3) | copy-start | bytes 1179652
  93.6 37.8 %copy-start.6 = (f32[16,3,2,1024]{3,0,2,1:T(8,128)}, f32[16,3,2,1024]{3,0,2,1:T(8,128)S(1)}, u32[]{:S(2)}) copy-start(f32[16,3,2,1024]{3,0,2,1:T(8,128)S(1)} %convolution_add_fusion.3) | copy-start | bytes 1179652
  180.2 6.2 %copy-start = (f32[1,3,2,16384]{3,2,1,0:T(2,128)S(1)}, f32[1,3,2,16384]{3,2,1,0:T(2,128)}, u32[]{:S(2)}) copy-start(f32[1,3,2,16384]{3,2,1,0:T(2,128)} %stack_reshape.4) | copy-start | bytes 1179652
  180.2 6.2 %copy-start.1 = (f32[1,3,2,16384]{3,2,1,0:T(2,128)S(1)}, f32[1,3,2,16384]{3,2,1,0:T(2,128)}, u32[]{:S(2)}) copy-start(f32[1,3,2,16384]{3,2,1,0:T(2,128)} %stack_reshape.5) | copy-start | bytes 1179652
  180.2 6.3 %copy-start.15 = (s32[2]{0:T(128)S(1)}, s32[2]{0:T(128)}, u32[]{:S(2)}) copy-start(s32[2]{0:T(128)} %get-tuple-element.47) | copy-start | bytes 28
  180.2 6.3 %copy-start.18 = (s32[2]{0:T(128)S(1)}, s32[2]{0:T(128)}, u32[]{:S(2)}) copy-start(s32[2]{0:T(128)} %get-tuple-element.46) | copy-start | bytes 28
  184.8 4.4 copy-start.4
  218.9 0.8 copy-start.13
  219.8 18.7 %copy-start.19 = (f32[5,2,16,1024]{3,2,1,0:T(8,128)S(1)}, f32[5,2,16,1024]{3,2,1,0:T(8,128)}, u32[]{:S(2)}) copy-start(f32[5,2,16,1024]{3,2,1,0:T(8,128)} %fusion.16) | copy-start | bytes 1966084
  238.5 20.3 %copy-start.12 = (f32[5,2,1024,16]{2,3,1,0:T(8,128)S(1)}, f32[5,2,1024,16]{2,3,1,0:T(8,128)}, u32[]{:S(2)}) copy-start(f32[5,2,1024,16]{2,3,1,0:T(8,128)} %constant_dynamic-update-slice_fusion) | copy-start | bytes 1966084
  303.2 34.8 %all-to-all-start.4 = ((f32[2,5,4,1,2,1,4,1024]{7,2,4,1,0,5,3,6:T(4,128)}), f32[2,5,4,1,2,1,4,1024]{7,2,4,1,0,5,3,6:T(4,128)S(1)}, u32[]{:S(2)}, u32[]{:S(2)}) async-start(f32[2,5,4,1,2,1,4,1024]{7,2,4,1,0,5,3,6:T(4,128)} %copy.110), calls=%async_computation.4 | async-start | bytes 2621440 | tf_op jit(solution)/shard_map/all_to_all | solution.py:162
  350.8 25.3 %copy-start.9 = (f32[16,1024]{1,0:T(8,128)S(1)}, f32[16,1024]{1,0:T(8,128)}, u32[]{:S(2)}) copy-start(f32[16,1024]{1,0:T(8,128)} %copy-done.8) | copy-start | bytes 196612
  350.8 25.3 %copy-start.11 = (f32[16,1024]{1,0:T(8,128)S(1)}, f32[16,1024]{1,0:T(8,128)}, u32[]{:S(2)}) copy-start(f32[16,1024]{1,0:T(8,128)} %copy-done.10) | copy-start | bytes 196612
  362.3 12.2 %all-to-all-start.6 = ((f32[2,1,1,4,2,4,1,1024]{7,4,5,0,6,2,1,3:T(2,128)}), f32[2,1,1,4,2,4,1,1024]{7,4,5,0,6,2,1,3:T(2,128)S(1)}, u32[]{:S(2)}, u32[]{:S(2)}) async-start(f32[2,1,1,4,2,4,1,1024]{7,4,5,0,6,2,1,3:T(2,128)} %copy.130), calls=%async_computation.6 | async-start | bytes 524288 | tf_op jit(solution)/shard_map/all_to_all | solution.py:146
  432.0 19.2 %copy-start.3 = (s32[16384]{0:T(1024)S(1)}, s32[16384]{0:T(1024)}, u32[]{:S(2)}) copy-start(s32[16384]{0:T(1024)} %copy-done.2) | copy-start | bytes 196612
  432.1 19.2 %copy-start.7 = (f32[2,16384]{1,0:T(2,128)S(1)}, f32[2,16384]{1,0:T(2,128)}, u32[]{:S(2)}) copy-start(f32[2,16384]{1,0:T(2,128)} %param.9) | copy-start | bytes 393220
  432.1 19.1 %copy-start.16 = (s32[2]{0:T(128)S(1)}, s32[2]{0:T(128)}, u32[]{:S(2)}) copy-start(s32[2]{0:T(128)} %get-tuple-element.47) | copy-start | bytes 28
  432.1 19.1 %copy-start.17 = (f32[2]{0:T(128)S(1)}, f32[2]{0:T(128)}, u32[]{:S(2)}) copy-start(f32[2]{0:T(128)} %get-tuple-element.45) | copy-start | bytes 28
where the time goes:
time: 579 us; the launch traced here: 572 us
  matrix products  342 us (59%)
  blocking collectives  70.2 us (12%)
  local copies, waits for them, and re-layouts  64.4 us (11%)
  waiting for transfers between devices  56.5 us (10%)
  starting transfers between devices  17.1 us (3%)
  other arithmetic  12.7 us (2%)
  between operations  8.9 us (2%)
    dot_general x16, matrix products, complex_einsum(): imag_out = jnp.einsum(formula, data_real, table_imag, precision=exact_mode)  86.3 us
    dot_general x15, matrix products, complex_einsum(): jnp.einsum(formula, data_imag, table_imag, precision=exact_mode)  86.3 us
    dot_general x16, matrix products, complex_einsum(): real_out = jnp.einsum(formula, data_real, table_real, precision=exact_mode)  85.9 us
    dot_general x15, matrix products, complex_einsum(): jnp.einsum(formula, data_imag, table_real, precision=exact_mode)  83.7 us
    all_to_all x1, waiting for transfers between devices, to_space(): lax.all_to_all(lax.all_to_all(shaped, 'rows', split_axis=5, concat_axis=2...  31 us
    all_to_all x2, blocking collectives, to_space(): lax.all_to_all(shaped, 'rows', split_axis=5, concat_axis=2, tiled=True)  28.1 us
    unnamed x51, local copies, waits for them, and re-layouts  26.6 us
    all_to_all x2, blocking collectives, to_frequency(): lax.all_to_all(shaped, 'rows', split_axis=2, concat_axis=5, tiled=True)  22.4 us
  transfers between devices with their start and end apart: 4, of which 4 were waited for; matrix products, arithmetic and copies ran while one was open for 1% of the time, Pallas kernels for 0%

commit v1 on v0

--- a/solution.py
+++ b/solution.py
@@ -6,6 +6,35 @@
 
 NC = 16384
 exact_mode = lax.Precision.HIGHEST
+
+
+def _cover_heads(xx, at_axis, in_array):
+    a_next = xx.shape
+    right_arr = xx.reshape(
+        *a_next[:at_axis], in_array, a_next[at_axis] // in_array, *a_next[at_axis + 1 :]
+    )
+    return jnp.moveaxis(right_arr, at_axis, 0)
+
+
+def slices_compute(u_in, axis_no):
+    step_out = list(u_in.shape[1:])
+    step_out[axis_no] *= u_in.shape[0]
+    return jnp.moveaxis(u_in, 0, axis_no).reshape(step_out)
+
+
+def remake_lanes(s0, along_axis, mat, piece_in):
+    a_now = lax.axis_size(along_axis)
+    parts_out = lax.axis_index(along_axis)
+    piece_now, res = (a_now, parts_out)
+    y1 = _cover_heads(s0, mat, piece_now)
+    r_now = y1
+    for tick in [*range(1, piece_now)]:
+        val2, row_out = ((res + tick) % piece_now, (res - tick) % piece_now)
+        piece_next = lax.dynamic_index_in_dim(y1, val2, 0)
+        earlier = tuple(((pp, (pp + tick) % piece_now) for pp in range(piece_now)))
+        value_now = lax.ppermute(piece_next, along_axis, earlier)
+        r_now = lax.dynamic_update_slice_in_dim(r_now, value_now, row_out, axis=0)
+    return slices_compute(r_now, piece_in)
 
 
 def split_factor(length):
@@ -143,12 +172,11 @@
         shaped = stacked.reshape(
             2, batch_len, rows_count, fields_count, local_rows, 1, 1, block_width
         )
-        arrived = lax.all_to_all(
+        arrived = remake_lanes(
             lax.all_to_all(shaped, "rows", split_axis=2, concat_axis=5, tiled=True),
             "fields",
-            split_axis=3,
-            concat_axis=6,
-            tiled=True,
+            3,
+            piece_in=6,
         )
         result = forward_columns(arrived.reshape(2, batch_len, local_rows, groups * block_width))
         return result

time: 579 us -> 574 us (level)
  blocking collectives: 70.2 us -> 57.9 us
  starting transfers between devices: 17.1 us -> 25.2 us
    all_to_all x2 -> x1, blocking collectives: 22.4 us -> 8.39 us  [to_frequency(): lax.all_to_all(shaped, 'rows', split_axis=2, concat_axis=5, tiled=True)]
    ppermute x0 -> x6, waiting for transfers between devices: none -> 13.6 us  [remake_lanes(): value_now = lax.ppermute(piece_next, along_axis, earlier)]
    all_to_all x2 -> x1, waiting for transfers between devices: 18.2 us -> 5.61 us  [to_frequency(): lax.all_to_all(shaped, 'rows', split_axis=2, concat_axis=5, tiled=True)]
    ppermute x0 -> x6, starting transfers between devices: none -> 10.2 us  [remake_lanes(): value_now = lax.ppermute(piece_next, along_axis, earlier)]
  transfers between devices with their start and end apart: 4 -> 9, of which waited for: 4 -> 7; matrix products, arithmetic and copies ran while one was open for 1% -> 1% of each run, Pallas kernels for 0% -> 0%
where the time goes in v1:
time: 574 us; the launch traced here: 566 us
  matrix products  342 us (60%)
  local copies, waits for them, and re-layouts  63.3 us (11%)
  blocking collectives  57.9 us (10%)
  waiting for transfers between devices  55.8 us (10%)
  starting transfers between devices  25.2 us (4%)
  other arithmetic  12.8 us (2%)
  between operations  8.93 us (2%)
    dot_general x16, matrix products, complex_einsum(): real_out = jnp.einsum(formula, data_real, table_real, precision=exact_mode)  86.7 us
    dot_general x16, matrix products, complex_einsum(): imag_out = jnp.einsum(formula, data_real, table_imag, precision=exact_mode)  86.5 us
    dot_general x15, matrix products, complex_einsum(): jnp.einsum(formula, data_imag, table_imag, precision=exact_mode)  85.7 us
    dot_general x15, matrix products, complex_einsum(): jnp.einsum(formula, data_imag, table_real, precision=exact_mode)  83.5 us
    all_to_all x1, waiting for transfers between devices, to_space(): lax.all_to_all(lax.all_to_all(shaped, 'rows', split_axis=5, concat_axis=2...  30.7 us
    all_to_all x2, blocking collectives, to_space(): lax.all_to_all(shaped, 'rows', split_axis=5, concat_axis=2, tiled=True)  28.1 us
    unnamed x51, local copies, waits for them, and re-layouts  26.6 us
    ppermute x6, waiting for transfers between devices, remake_lanes(): value_now = lax.ppermute(piece_next, along_axis, earlier)  13.6 us
  transfers between devices with their start and end apart: 9, of which 7 were waited for; matrix products, arithmetic and copies ran while one was open for 1% of the time, Pallas kernels for 0%

profile of v1, /device:TPU:0, one launch (start us, length us, event | category | flops | bytes accessed | tf_op | source)
XLA Modules:
  0.0 566.3 jit_solution(219127687024121948)
XLA Ops:
  0.0 6.7 %copy.84 = f32[3,8,4096]{1,0,2:T(4,128)} copy(f32[3,8,4096]{2,1,0:T(8,128)} %param.5) | data formatting | bytes 786432 | tf_op args[0]
  6.7 7.5 %reshape.1882 = f32[4,1,24576]{2,1,0:T(1,128)} reshape(f32[4096,3,8]{2,1,0:T(4,128)} %bitcast.483) | data formatting | bytes 786432
  14.2 4.3 all-to-all-start
  20.1 5.8 %all-to-all-done = f32[4,1,24576]{2,1,0:T(1,128)S(1)} async-done(((f32[4,1,24576]{2,1,0:T(1,128)}), f32[4,1,24576]{2,1,0:T(1,128)S(1)}, u32[]{:S(2)}, u32[]{:S(2)}) %all-to-all-start) | async-done | bytes 393248 | tf_op jit(solution)/shard_map/all_to_all | solution.py:202
  28.2 8.8 %reshape.1883 = f32[4096,3,8]{2,1,0:T(4,128)} reshape(f32[4,24576]{1,0:T(4,128)S(1)} %reduce) | data formatting | bytes 786432
  36.9 6.7 %copy.168 = f32[3,8,4,1024]{3,2,1,0:T(4,128)S(1)} copy(f32[3,8,4,1024]{1,0,3,2:T(4,128)} %bitcast.482) | data formatting | bytes 786432 | tf_op jit(solution)/shard_map/all_to_all | solution.py:202
  50.8 3.5 all-to-all-start.1
  60.3 5.6 all-to-all-done.1
  76.1 7.2 %collective-permute-done.1 = f32[1,2,3,1,1,2,4,1,1024]{8,5,0,2,1,6,7,4,3:T(2,128)S(1)} collective-permute-done((f32[1,2,3,1,1,2,4,1,1024]{8,5,0,2,1,6,7,4,3:T(2,128)S(1)}, f32[1,2,3,1,1,2,4,1,1024]{8,5,0,2,1,6,7,4,3:T(2,128)S(1)}, u32[]{:S(2)}, u32[]{:S(2)}) %collective-permute-start.1) | collective-permute-done | bytes 196640 | tf_op jit(solution)/shard_map/ppermute | solution.py:35
  86.2 19.1 %fusion.24 = f32[1024,3,2,16]{0,3,2,1:T(8,128)S(1)} fusion(f32[16,3,2,1024]{3,0,2,1:T(8,128)S(1)} %convolution_add_fusion.3, f32[16,3,2,1024]{3,0,2,1:T(8,128)S(1)} %convolution_subtract_fusion.3, f32[16,1024]{1,0:T(8,128)S(1)} %get-tuple-element.58, f32[16,1024]{1,0:T(8,128)S(1)} %get-tuple-element.59), kind=kOutput, calls=%fused_computation.27 | convolution fusion | flops 1222934528 | bytes 1310720 | tf_op jit(solution)/shard_map/brkc,cq->brqk/dot_general | solution.py:57
  105.3 19.0 %fusion.22 = f32[1024,3,2,16]{0,3,2,1:T(8,128)} fusion(f32[16,3,2,1024]{3,0,2,1:T(8,128)S(1)} %convolution_add_fusion.3, f32[16,3,2,1024]{3,0,2,1:T(8,128)S(1)} %convolution_subtract_fusion.3, f32[16,1024]{1,0:T(8,128)S(1)} %get-tuple-element.58, f32[16,1024]{1,0:T(8,128)S(1)} %get-tuple-element.59), kind=kOutput, calls=%fused_computation.25 | convolution fusion | flops 1222934528 | bytes 1310720 | tf_op jit(solution)/shard_map/brkc,cq->brqk/dot_general | solution.py:61
  124.4 19.4 %fusion.88 = f32[3,2,1024,16]{2,3,1,0:T(8,128)} fusion(f32[1024,3,2,16]{0,3,2,1:T(8,128)S(1)} %fusion.24, f32[16,3,2,1024]{3,0,2,1:T(8,128)S(1)} %convolution_add_fusion.3, f32[16,3,2,1024]{3,0,2,1:T(8,128)S(1)} %convolution_subtract_fusion.3, f32[16,1024]{1,0:T(8,128)S(1)} %get-tuple-element.58, f32[16,1024]{1,0:T(8,128)S(1)} %get-tuple-element.59), kind=kOutput, calls=%fused_computation.84 | convolution fusion | flops 1223032832 | bytes 1703936 | tf_op jit(solution)/shard_map/brkc,cq->brqk/dot_general | solution.py:60
  148.1 20.5 %fusion.94 = f32[3,2,1024,16]{2,3,1,0:T(8,128)} fusion(f32[1024,3,2,16]{0,3,2,1:T(8,128)} %fusion.22, f32[16,3,2,1024]{3,0,2,1:T(8,128)} %copy-done.6, f32[16,3,2,1024]{3,0,2,1:T(8,128)} %copy-done.5, f32[16,1024]{1,0:T(8,128)} %copy-done.8, f32[16,1024]{1,0:T(8,128)} %copy-done.10), kind=kOutput, calls=%fused_computation.86 | convolution fusion | flops 1223032832 | bytes 1703936 | tf_op jit(solution)/shard_map/brkc,cq->brqk/dot_general | solution.py:58
  188.4 20.5 %fusion.16 = f32[5,2,16,1024]{3,2,1,0:T(8,128)} fusion(f32[5,2,1024,16]{2,3,1,0:T(8,128)} %constant_dynamic-update-slice_fusion), kind=kOutput, calls=%fused_computation.19 | convolution fusion | flops 2027945984 | bytes 1310720 | tf_op jit(solution)/shard_map/brqk,qc->brkc/dot_general | solution.py:57
  213.0 18.7 %fusion.14 = f32[5,2,16,1024]{3,2,1,0:T(8,128)S(1)} fusion(f32[5,2,1024,16]{2,3,1,0:T(8,128)S(1)} %constant_dynamic-update-slice_fusion.5), kind=kOutput, calls=%fused_computation.17 | convolution fusion | flops 2027945984 | bytes 1310720 | tf_op jit(solution)/shard_map/brqk,qc->brkc/dot_general | solution.py:61
  231.7 19.9 %fusion.77 = f32[5,2,16,1024]{3,2,1,0:T(8,128)S(1)} fusion(f32[5,2,16,1024]{3,2,1,0:T(8,128)S(1)} %copy-done.19, f32[5,2,1024,16]{2,3,1,0:T(8,128)} %copy-done.13), kind=kOutput, calls=%fused_computation.75 | convolution fusion | flops 2028109824 | bytes 1966080 | tf_op jit(solution)/shard_map/brqk,qc->brkc/dot_general | solution.py:60
  251.6 18.9 %fusion.80 = f32[5,2,16,1024]{3,2,1,0:T(8,128)S(1)} fusion(f32[5,2,16,1024]{3,2,1,0:T(8,128)S(1)} %fusion.14, f32[5,2,1024,16]{2,3,1,0:T(8,128)S(1)} %copy-done.12), kind=kOutput, calls=%fused_computation.76 | convolution fusion | flops 2028109824 | bytes 1966080 | tf_op jit(solution)/shard_map/brqk,qc->brkc/dot_general | solution.py:58
  274.6 19.7 %all_to_all.129 = f32[2,5,1,1,2,4,4,1024]{7,6,4,1,3,2,0,5:T(4,128)S(1)} all-to-all(f32[2,5,1,1,2,4,4,1024]{7,6,4,1,3,2,0,5:T(4,128)S(1)} %copy.169), channel_id=1, replica_groups=mesh['sims'=2,'rows'=4,'fields'=4] {'rows'}, dimensions={5} | all-to-all | bytes 2621440 | tf_op jit(solution)/shard_map/all_to_all | solution.py:191
  296.2 7.2 %all-to-all-start.3 = ((f32[2,5,4,1,2,1,4,1024]{7,2,4,1,0,5,3,6:T(4,128)}), f32[2,5,4,1,2,1,4,1024]{7,2,4,1,0,5,3,6:T(4,128)S(1)}, u32[]{:S(2)}, u32[]{:S(2)}) async-start(f32[2,5,4,1,2,1,4,1024]{7,2,4,1,0,5,3,6:T(4,128)} %copy.109), calls=%async_computation.3 | async-start | bytes 2621440 | tf_op jit(solution)/shard_map/all_to_all | solution.py:190
  303.5 30.7 %all-to-all-done.3 = f32[2,5,4,1,2,1,4,1024]{7,2,4,1,0,5,3,6:T(4,128)S(1)} async-done(((f32[2,5,4,1,2,1,4,1024]{7,2,4,1,0,5,3,6:T(4,128)}), f32[2,5,4,1,2,1,4,1024]{7,2,4,1,0,5,3,6:T(4,128)S(1)}, u32[]{:S(2)}, u32[]{:S(2)}) %all-to-all-start.3) | async-done | bytes 1310752 | tf_op jit(solution)/shard_map/all_to_all | solution.py:190
  349.5 8.4 %all_to_all.130 = f32[2,1,4,4,2,1,1,1024]{7,4,3,6,5,1,0,2:T(2,128)S(1)} all-to-all(f32[2,1,4,4,2,1,1,1024]{7,4,3,6,5,1,0,2:T(2,128)S(1)} %copy.128), channel_id=1, replica_groups=mesh['sims'=2,'rows'=4,'fields'=4] {'rows'}, dimensions={2} | all-to-all | bytes 524288 | tf_op jit(solution)/shard_map/all_to_all | solution.py:176
  368.6 18.3 %fusion.12 = f32[1024,2,16]{0,2,1:T(8,128)S(1)} fusion(f32[16,1,2,1024]{3,0,2,1:T(8,128)S(1)} %fusion.97, f32[16,1,2,1024]{3,0,2,1:T(8,128)S(1)} %fusion.98, f32[16,1024]{1,0:T(8,128)S(1)} %copy-done.9, f32[16,1024]{1,0:T(8,128)S(1)} %copy-done.11), kind=kOutput, calls=%fused_computation.15 | convolution fusion | flops 417431552 | bytes 524288 | tf_op jit(solution)/shard_map/brkc,cq->brqk/dot_general | solution.py:60
  387.0 18.3 %fusion.10 = f32[1024,2,16]{0,2,1:T(8,128)S(1)} fusion(f32[16,1,2,1024]{3,0,2,1:T(8,128)S(1)} %fusion.97, f32[16,1,2,1024]{3,0,2,1:T(8,128)S(1)} %fusion.98, f32[16,1024]{1,0:T(8,128)S(1)} %copy-done.9, f32[16,1024]{1,0:T(8,128)S(1)} %copy-done.11), kind=kOutput, calls=%fused_computation.13 | convolution fusion | flops 417431552 | bytes 524288 | tf_op jit(solution)/shard_map/brkc,cq->brqk/dot_general | solution.py:58
  405.3 18.4 %fusion.114 = f32[1,2,1024,16]{2,3,1,0:T(8,128)S(1)} fusion(f32[1024,2,16]{0,2,1:T(8,128)S(1)} %fusion.12, f32[16,1,2,1024]{3,0,2,1:T(8,128)S(1)} %fusion.97, f32[16,1,2,1024]{3,0,2,1:T(8,128)S(1)} %fusion.98, f32[16,1024]{1,0:T(8,128)S(1)} %copy-done.9, f32[16,1024]{1,0:T(8,128)S(1)} %copy-done.11), kind=kOutput, calls=%fused_computation.110 | convolution fusion | flops 417464320 | bytes 655360 | tf_op jit(solution)/shard_map/brkc,cq->brqk/dot_general | solution.py:57
  424.6 18.2 %fusion.120 = f32[1,2,1024,16]{2,3,1,0:T(8,128)S(1)} fusion(f32[1024,2,16]{0,2,1:T(8,128)S(1)} %fusion.10, f32[16,1,2,1024]{3,0,2,1:T(8,128)S(1)} %fusion.97, f32[16,1,2,1024]{3,0,2,1:T(8,128)S(1)} %fusion.98, f32[16,1024]{1,0:T(8,128)S(1)} %copy-done.9, f32[16,1024]{1,0:T(8,128)S(1)} %copy-done.11), kind=kOutput, calls=%fused_computation.112 | convolution fusion | flops 417464320 | bytes 655360 | tf_op jit(solution)/shard_map/brkc,cq->brqk/dot_general | solution.py:61
  444.5 21.4 %fusion.4 = f32[2,16,1024]{2,1,0:T(8,128)S(1)} fusion(f32[2,1024,16]{2,1,0:T(8,128)S(1)} %reshape.1845), kind=kOutput, calls=%fused_computation.7 | convolution fusion | flops 417333248 | bytes 262144 | tf_op jit(solution)/shard_map/brqk,qc->brkc/dot_general | solution.py:60
  466.3 21.2 %fusion.2 = f32[2,16,1024]{2,1,0:T(8,128)S(1)} fusion(f32[2,1024,16]{2,1,0:T(8,128)S(1)} %reshape.1844), kind=kOutput, calls=%fused_computation.5 | convolution fusion | flops 417333248 | bytes 262144 | tf_op jit(solution)/shard_map/brqk,qc->brkc/dot_general | solution.py:58
  487.5 21.5 %fusion.105 = f32[2,16,1024]{2,1,0:T(8,128)S(1)} fusion(f32[2,16,1024]{2,1,0:T(8,128)S(1)} %fusion.4, f32[2,1024,16]{2,1,0:T(8,128)S(1)} %reshape.1844), kind=kOutput, calls=%fused_computation.107 | convolution fusion | flops 417366016 | bytes 393216 | tf_op jit(solution)/shard_map/brqk,qc->brkc/dot_general | solution.py:57
  508.9 21.1 %fusion.108 = f32[2,16,1024]{2,1,0:T(8,128)S(1)} fusion(f32[2,16,1024]{2,1,0:T(8,128)S(1)} %fusion.2, f32[2,1024,16]{2,1,0:T(8,128)S(1)} %reshape.1845), kind=kOutput, calls=%fused_computation.108 | convolution fusion | flops 417366016 | bytes 393216 | tf_op jit(solution)/shard_map/brqk,qc->brkc/dot_general | solution.py:61
  531.7 8.4 %all_to_all.131 = f32[2,1,1,1,2,4,4,1024]{7,6,4,3,2,1,0,5:T(4,128)S(1)} all-to-all(f32[2,1,1,1,2,4,4,1024]{7,6,4,3,2,1,0,5:T(4,128)S(1)} %copy.172), channel_id=1, replica_groups=mesh['sims'=2,'rows'=4,'fields'=4] {'rows'}, dimensions={5} | all-to-all | bytes 524288 | tf_op jit(solution)/shard_map/all_to_all | solution.py:191
  540.3 13.1 %all_to_all.132 = f32[2,1,4,1,2,1,4,1024]{7,2,4,0,5,3,1,6:T(4,128)S(1)} all-to-all(f32[2,1,4,1,2,1,4,1024]{7,2,4,0,5,3,1,6:T(4,128)S(1)} %copy.139), channel_id=1, replica_groups=mesh['sims'=2,'rows'=4,'fields'=4] {'fields'}, dimensions={6} | all-to-all | bytes 524288 | tf_op jit(solution)/shard_map/all_to_all | solution.py:190
  557.0 8.4 %all_to_all.133 = f32[2,32,1024]{2,0,1:T(2,128)S(1)} all-to-all(f32[2,32,1024]{2,0,1:T(2,128)S(1)} %copy.146), channel_id=1, replica_groups=mesh['sims'=2,'rows'=4,'fields'=4] {'rows'}, dimensions={1} | all-to-all | bytes 524288 | tf_op jit(solution)/shard_map/all_to_all | solution.py:282
  (208 shorter events, 91.1 us)
Async XLA Ops:
  6.7 12.4 %copy-start.14 = (s32[6]{0:T(128)S(1)}, s32[6]{0:T(128)}, u32[]{:S(2)}) copy-start(s32[6]{0:T(128)} %param.6) | copy-start | bytes 76
  14.2 11.7 %all-to-all-start = ((f32[4,1,24576]{2,1,0:T(1,128)}), f32[4,1,24576]{2,1,0:T(1,128)S(1)}, u32[]{:S(2)}, u32[]{:S(2)}) async-start(f32[4,1,24576]{2,1,0:T(1,128)} %reshape.1882), calls=%async_computation | async-start | bytes 786432 | tf_op jit(solution)/shard_map/all_to_all | solution.py:202
  20.1 104.3 %copy-start.8 = (f32[16,1024]{1,0:T(8,128)}, f32[16,1024]{1,0:T(8,128)S(1)}, u32[]{:S(2)}) copy-start(f32[16,1024]{1,0:T(8,128)S(1)} %get-tuple-element.58) | copy-start | bytes 196612
  20.1 104.3 %copy-start.10 = (f32[16,1024]{1,0:T(8,128)}, f32[16,1024]{1,0:T(8,128)S(1)}, u32[]{:S(2)}) copy-start(f32[16,1024]{1,0:T(8,128)S(1)} %get-tuple-element.59) | copy-start | bytes 196612
  50.8 15.1 %all-to-all-start.1 = ((f32[2,3,4,4,2,1,1,1024]{7,4,3,1,6,5,0,2:T(2,128)}), f32[2,3,4,4,2,1,1,1024]{7,4,3,1,6,5,0,2:T(2,128)S(1)}, u32[]{:S(2)}, u32[]{:S(2)}) async-start(f32[2,3,4,4,2,1,1,1024]{7,4,3,1,6,5,0,2:T(2,128)} %copy.92), calls=%async_computation.1 | async-start | bytes 1572864 | tf_op jit(solution)/shard_map/all_to_all | solution.py:176
  60.3 119.1 %copy-start.2 = (s32[16384]{0:T(1024)}, s32[16384]{0:T(1024)S(1)}, u32[]{:S(2)}) copy-start(s32[16384]{0:T(1024)S(1)} %get-tuple-element.62) | copy-start | bytes 196612
  65.9 10.2 %collective-permute-start = (f32[1,2,3,1,1,2,4,1,1024]{8,5,0,2,1,6,7,4,3:T(2,128)S(1)}, f32[1,2,3,1,1,2,4,1,1024]{8,5,0,2,1,6,7,4,3:T(2,128)S(1)}, u32[]{:S(2)}, u32[]{:S(2)}) collective-permute-start(f32[1,2,3,1,1,2,4,1,1024]{8,5,0,2,1,6,7,4,3:T(2,128)S(1)} %get-tuple-element.25), channel_id=1, source_target_pairs={{0,1},{1,2},{2,3},{3,0},{4,5},{5,6},{6,7},{7,4},{8,9},{9,10},{10,1... | collective-permute-start | bytes 589832 | tf_op jit(solution)/shard_map/ppermute | solution.py:35
  68.2 15.1 %collective-permute-start.1 = (f32[1,2,3,1,1,2,4,1,1024]{8,5,0,2,1,6,7,4,3:T(2,128)S(1)}, f32[1,2,3,1,1,2,4,1,1024]{8,5,0,2,1,6,7,4,3:T(2,128)S(1)}, u32[]{:S(2)}, u32[]{:S(2)}) collective-permute-start(f32[1,2,3,1,1,2,4,1,1024]{8,5,0,2,1,6,7,4,3:T(2,128)S(1)} %get-tuple-element.24), channel_id=1, source_target_pairs={{0,2},{1,3},{2,0},{3,1},{4,6},{5,7},{6,4},{7,5},{8,10},{9,11},{10,... | collective-permute-start | bytes 589832 | tf_op jit(solution)/shard_map/ppermute | solution.py:35
  71.3 12.1 %collective-permute-start.2 = (f32[1,2,3,1,1,2,4,1,1024]{8,5,0,2,1,6,7,4,3:T(2,128)S(1)}, f32[1,2,3,1,1,2,4,1,1024]{8,5,0,2,1,6,7,4,3:T(2,128)S(1)}, u32[]{:S(2)}, u32[]{:S(2)}) collective-permute-start(f32[1,2,3,1,1,2,4,1,1024]{8,5,0,2,1,6,7,4,3:T(2,128)S(1)} %get-tuple-element.23), channel_id=1, source_target_pairs={{0,3},{1,0},{2,1},{3,2},{4,7},{5,4},{6,5},{7,6},{8,11},{9,8},{10,9... | collective-permute-start | bytes 589832 | tf_op jit(solution)/shard_map/ppermute | solution.py:35
  85.7 38.7 %copy-start.5 = (f32[16,3,2,1024]{3,0,2,1:T(8,128)}, f32[16,3,2,1024]{3,0,2,1:T(8,128)S(1)}, u32[]{:S(2)}) copy-start(f32[16,3,2,1024]{3,0,2,1:T(8,128)S(1)} %convolution_subtract_fusion.3) | copy-start | bytes 1179652
  86.2 38.2 %copy-start.6 = (f32[16,3,2,1024]{3,0,2,1:T(8,128)}, f32[16,3,2,1024]{3,0,2,1:T(8,128)S(1)}, u32[]{:S(2)}) copy-start(f32[16,3,2,1024]{3,0,2,1:T(8,128)S(1)} %convolution_add_fusion.3) | copy-start | bytes 1179652
  173.2 6.2 %copy-start = (f32[1,3,2,16384]{3,2,1,0:T(2,128)S(1)}, f32[1,3,2,16384]{3,2,1,0:T(2,128)}, u32[]{:S(2)}) copy-start(f32[1,3,2,16384]{3,2,1,0:T(2,128)} %stack_reshape.4) | copy-start | bytes 1179652
  173.2 6.3 %copy-start.1 = (f32[1,3,2,16384]{3,2,1,0:T(2,128)S(1)}, f32[1,3,2,16384]{3,2,1,0:T(2,128)}, u32[]{:S(2)}) copy-start(f32[1,3,2,16384]{3,2,1,0:T(2,128)} %stack_reshape.5) | copy-start | bytes 1179652
  173.2 6.3 %copy-start.15 = (s32[2]{0:T(128)S(1)}, s32[2]{0:T(128)}, u32[]{:S(2)}) copy-start(s32[2]{0:T(128)} %get-tuple-element.57) | copy-start | bytes 28
  173.2 6.3 %copy-start.18 = (s32[2]{0:T(128)S(1)}, s32[2]{0:T(128)}, u32[]{:S(2)}) copy-start(s32[2]{0:T(128)} %get-tuple-element.56) | copy-start | bytes 28
  177.7 4.4 copy-start.4
  212.1 0.9 copy-start.13
  213.0 18.7 %copy-start.19 = (f32[5,2,16,1024]{3,2,1,0:T(8,128)S(1)}, f32[5,2,16,1024]{3,2,1,0:T(8,128)}, u32[]{:S(2)}) copy-start(f32[5,2,16,1024]{3,2,1,0:T(8,128)} %fusion.16) | copy-start | bytes 1966084
  231.7 19.9 %copy-start.12 = (f32[5,2,1024,16]{2,3,1,0:T(8,128)S(1)}, f32[5,2,1024,16]{2,3,1,0:T(8,128)}, u32[]{:S(2)}) copy-start(f32[5,2,1024,16]{2,3,1,0:T(8,128)} %constant_dynamic-update-slice_fusion) | copy-start | bytes 1966084
  296.2 38.0 %all-to-all-start.3 = ((f32[2,5,4,1,2,1,4,1024]{7,2,4,1,0,5,3,6:T(4,128)}), f32[2,5,4,1,2,1,4,1024]{7,2,4,1,0,5,3,6:T(4,128)S(1)}, u32[]{:S(2)}, u32[]{:S(2)}) async-start(f32[2,5,4,1,2,1,4,1024]{7,2,4,1,0,5,3,6:T(4,128)} %copy.109), calls=%async_computation.3 | async-start | bytes 2621440 | tf_op jit(solution)/shard_map/all_to_all | solution.py:190
  345.3 23.3 %copy-start.9 = (f32[16,1024]{1,0:T(8,128)S(1)}, f32[16,1024]{1,0:T(8,128)}, u32[]{:S(2)}) copy-start(f32[16,1024]{1,0:T(8,128)} %copy-done.8) | copy-start | bytes 196612
  345.3 23.3 %copy-start.11 = (f32[16,1024]{1,0:T(8,128)S(1)}, f32[16,1024]{1,0:T(8,128)}, u32[]{:S(2)}) copy-start(f32[16,1024]{1,0:T(8,128)} %copy-done.10) | copy-start | bytes 196612
  357.9 6.4 %collective-permute-start.3 = (f32[1,2,1,1,1,2,4,1,1024]{8,5,0,1,6,7,4,3,2:T(2,128)S(1)}, f32[1,2,1,1,1,2,4,1,1024]{8,5,0,1,6,7,4,3,2:T(2,128)S(1)}, u32[]{:S(2)}, u32[]{:S(2)}) collective-permute-start(f32[1,2,1,1,1,2,4,1,1024]{8,5,0,1,6,7,4,3,2:T(2,128)S(1)} %get-tuple-element.42), channel_id=1, source_target_pairs={{0,1},{1,2},{2,3},{3,0},{4,5},{5,6},{6,7},{7,4},{8,9},{9,10},{10,1... | collective-permute-start | bytes 196616 | tf_op jit(solution)/shard_map/ppermute | solution.py:35
  360.3 6.7 %collective-permute-start.4 = (f32[1,2,1,1,1,2,4,1,1024]{8,5,0,1,6,7,4,3,2:T(2,128)S(1)}, f32[1,2,1,1,1,2,4,1,1024]{8,5,0,1,6,7,4,3,2:T(2,128)S(1)}, u32[]{:S(2)}, u32[]{:S(2)}) collective-permute-start(f32[1,2,1,1,1,2,4,1,1024]{8,5,0,1,6,7,4,3,2:T(2,128)S(1)} %get-tuple-element.41), channel_id=1, source_target_pairs={{0,2},{1,3},{2,0},{3,1},{4,6},{5,7},{6,4},{7,5},{8,10},{9,11},{10,... | collective-permute-start | bytes 196616 | tf_op jit(solution)/shard_map/ppermute | solution.py:35
  362.4 4.9 collective-permute-start.5
  424.6 19.2 %copy-start.3 = (s32[16384]{0:T(1024)S(1)}, s32[16384]{0:T(1024)}, u32[]{:S(2)}) copy-start(s32[16384]{0:T(1024)} %copy-done.2) | copy-start | bytes 196612
  424.6 19.2 %copy-start.7 = (f32[2,16384]{1,0:T(2,128)S(1)}, f32[2,16384]{1,0:T(2,128)}, u32[]{:S(2)}) copy-start(f32[2,16384]{1,0:T(2,128)} %param.9) | copy-start | bytes 393220
  424.6 19.1 %copy-start.16 = (s32[2]{0:T(128)S(1)}, s32[2]{0:T(128)}, u32[]{:S(2)}) copy-start(s32[2]{0:T(128)} %get-tuple-element.57) | copy-start | bytes 28
  424.6 19.1 %copy-start.17 = (f32[2]{0:T(128)S(1)}, f32[2]{0:T(128)}, u32[]{:S(2)}) copy-start(f32[2]{0:T(128)} %get-tuple-element.55) | copy-start | bytes 28
